TPU v7x, 32 devices: a 4x4x1 block of a 4x4x8 slice. The times are simulated.
32 devices in a mesh: dp: 1 (over z), tp: 4 (over y), cp: 8 (over x, core).
Axes of the slice: x: 4, y: 4, z: 1, core: 2. Of those that a mesh axis runs over, the one named last changes fastest.
The devices are a block of a 4x4x8 slice.
Arguments:
- x_chunk: bfloat16 [24, 512, 3072], P('dp', 'cp')
- w_query: bfloat16 [3072, 3072], P(None, 'tp')
- w_key: bfloat16 [3072, 1024], P(None, 'tp')
- w_value: bfloat16 [3072, 1024], P(None, 'tp')
- w_out: bfloat16 [3072, 3072], P('tp')
- q_gain: bfloat16 [3072], P('tp')
- k_gain: bfloat16 [1024], P('tp')
- post_gain: bfloat16 [3072], replicated
- cache_k: bfloat16 [24, 8192, 8, 128], P('dp', 'cp', 'tp')
- cache_v: bfloat16 [24, 8192, 8, 128], P('dp', 'cp', 'tp')
- prefix_len: int32 [24], P('dp')
Outputs:
- output 1: bfloat16 [24, 512, 3072], P('dp', 'cp')
- output 2: bfloat16 [24, 512, 8, 128], P('dp', 'cp', 'tp')
- output 3: bfloat16 [24, 512, 8, 128], P('dp', 'cp', 'tp')
All inputs are finite; a program needn't handle non-finite values.
Results may differ from a plain program's by a relative error of at most 0.00713331.
Values are sent between devices in bfloat16 or wider.
A program may use at most 768 MiB of HBM per device.

v0:
```python
import jax
import jax.numpy as jnp
from jax import lax
from jax.sharding import PartitionSpec as P

NORM_EPS = 1e-6
ROPE_BASE = 500000.0
MASK_VALUE = -1e30


def rope_apply(head_vals, positions):
    head_dim = head_vals.shape[-1]
    half_dim = head_dim // 2
    inv_freq = ROPE_BASE ** (-(jnp.arange(half_dim, dtype=jnp.float32) * 2.0 / head_dim))
    angles = positions.astype(jnp.float32)[..., None] * inv_freq
    cos_tab = jnp.cos(angles)[..., None, :]
    sin_tab = jnp.sin(angles)[..., None, :]
    first_half = head_vals[..., :half_dim]
    second_half = head_vals[..., half_dim:]
    return jnp.concatenate([first_half * cos_tab - second_half * sin_tab, second_half * cos_tab + first_half * sin_tab], axis=-1)


def solution(mesh):
    cp_size = mesh.shape['cp']
    tp_size = mesh.shape['tp']

    def local_step(x_chunk, w_query, w_key, w_value, w_out, q_gain, k_gain, post_gain, cache_k, cache_v, prefix_len):
        batch_rows, chunk_dev, model_dim = x_chunk.shape
        cache_dev = cache_k.shape[1]
        kv_local = cache_k.shape[2]
        head_dim = cache_k.shape[3]
        q_local = w_query.shape[1] // head_dim
        groups = q_local // kv_local
        cp_index = lax.axis_index('cp')
        tokens = x_chunk.reshape(batch_rows * chunk_dev, model_dim)
        q_raw = jnp.dot(tokens, w_query, preferred_element_type=jnp.float32)
        k_raw = jnp.dot(tokens, w_key, preferred_element_type=jnp.float32)
        v_raw = jnp.dot(tokens, w_value, preferred_element_type=jnp.float32)
        square_sums = lax.psum(jnp.stack([jnp.sum(q_raw * q_raw, axis=-1), jnp.sum(k_raw * k_raw, axis=-1)]), 'tp')
        q_inv = lax.rsqrt(square_sums[0] / (w_query.shape[1] * tp_size) + NORM_EPS)
        k_inv = lax.rsqrt(square_sums[1] / (w_key.shape[1] * tp_size) + NORM_EPS)
        q_norm = (q_raw * q_inv[:, None] * q_gain.astype(jnp.float32)).reshape(batch_rows, chunk_dev, q_local, head_dim)
        k_norm = (k_raw * k_inv[:, None] * k_gain.astype(jnp.float32)).reshape(batch_rows, chunk_dev, kv_local, head_dim)
        positions = prefix_len[:, None] + cp_index * chunk_dev + jnp.arange(chunk_dev, dtype=jnp.int32)[None, :]
        q_new = rope_apply(q_norm, positions).astype(jnp.bfloat16).reshape(batch_rows, chunk_dev, kv_local, groups, head_dim)
        chunk_k = rope_apply(k_norm, positions).astype(jnp.bfloat16)
        chunk_v = v_raw.astype(jnp.bfloat16).reshape(batch_rows, chunk_dev, kv_local, head_dim)
        q_all = lax.all_gather(q_new, 'cp', axis=1, tiled=True)
        score_scale = head_dim ** -0.5
        slot_index = cp_index * cache_dev + jnp.arange(cache_dev)
        cache_ok = (slot_index[None, :] < prefix_len[:, None])[:, None, None, None, :]
        key_index = cp_index * chunk_dev + jnp.arange(chunk_dev)

        def block_attention(block_id):
            q_blk = lax.dynamic_slice_in_dim(q_all, block_id * chunk_dev, chunk_dev, axis=1)
            query_index = block_id * chunk_dev + jnp.arange(chunk_dev)
            chunk_ok = (key_index[None, :] <= query_index[:, None])[None, :, None, None, :]
            s_cache = jnp.einsum('bqkgd,btkd->bqkgt', q_blk, cache_k, preferred_element_type=jnp.float32) * score_scale
            s_cache = jnp.where(cache_ok, s_cache, MASK_VALUE)
            s_chunk = jnp.einsum('bqkgd,btkd->bqkgt', q_blk, chunk_k, preferred_element_type=jnp.float32) * score_scale
            s_chunk = jnp.where(chunk_ok, s_chunk, MASK_VALUE)
            row_max = jnp.maximum(jnp.max(s_cache, axis=-1), jnp.max(s_chunk, axis=-1))
            p_cache = jnp.exp(s_cache - row_max[..., None])
            p_chunk = jnp.exp(s_chunk - row_max[..., None])
            den_sum = jnp.sum(p_cache, axis=-1) + jnp.sum(p_chunk, axis=-1)
            num_sum = jnp.einsum('bqkgt,btkd->bqkgd', p_cache.astype(jnp.bfloat16), cache_v, preferred_element_type=jnp.float32)
            num_sum = num_sum + jnp.einsum('bqkgt,btkd->bqkgd', p_chunk.astype(jnp.bfloat16), chunk_v, preferred_element_type=jnp.float32)
            return row_max, den_sum, num_sum

        part_max, part_den, part_num = lax.map(block_attention, jnp.arange(cp_size))
        glob_max = lax.pmax(part_max, 'cp')
        factor = jnp.exp(part_max - glob_max)
        den_total = lax.psum_scatter(part_den * factor, 'cp', scatter_dimension=0, tiled=False)
        num_total = lax.psum_scatter(part_num * factor[..., None], 'cp', scatter_dimension=0, tiled=False)
        attn_out = (num_total / den_total[..., None]).astype(jnp.bfloat16).reshape(batch_rows * chunk_dev, q_local * head_dim)
        mixed_part = jnp.dot(attn_out, w_out, preferred_element_type=jnp.float32)
        mixed_sum = lax.psum(mixed_part, 'tp')
        normed = mixed_sum * lax.rsqrt(jnp.mean(mixed_sum * mixed_sum, axis=-1, keepdims=True) + NORM_EPS) * post_gain.astype(jnp.float32)
        block_out = (x_chunk.astype(jnp.float32) + normed.reshape(batch_rows, chunk_dev, model_dim)).astype(jnp.bfloat16)
        return block_out, chunk_k, chunk_v

    x_spec = P('dp', 'cp', None)
    head_spec = P('dp', 'cp', 'tp', None)
    in_specs = (x_spec, P(None, 'tp'), P(None, 'tp'), P(None, 'tp'), P('tp', None), P('tp'), P('tp'), P(None), head_spec, head_spec, P('dp'))
    out_specs = (x_spec, head_spec, head_spec)
    return jax.shard_map(local_step, mesh=mesh, in_specs=in_specs, out_specs=out_specs, check_vma=False)
```

profile of v0, /device:TPU:97, one launch (start us, length us, event | category | flops | bytes accessed | tf_op | source)
XLA Modules:
  0.0 1415.2 jit_solution(9931744745924441114)
XLA Ops:
  8.1 13.2 multiply_reduce_fusion.1
  25.2 16.5 %psum.14 = f32[2,1536]{1,0:T(2,128)S(1)} all-reduce(f32[2,1536]{1,0:T(2,128)S(1)} %pad_maximum_fusion.2), channel_id=1, replica_groups=mesh['dp'=1,'tp'=4,'cp'=8] {'tp'}, use_global_device_ids=true, to_apply=%region_2.0 | all-reduce | flops 3072 | bytes 24576 | tf_op jit(solution)/shard_map/psum | solution.py:39
  73.6 11.6 copy.65
  93.7 12.3 copy.67
  109.2 59.3 %all-gather.2.cloned.1.call-done = bf16[24,512,2,3,128]{4,1,3,2,0:T(8,128)(2,1)} async-done(((bf16[24,64,2,3,128]{4,1,3,2,0:T(8,128)(2,1)}), bf16[24,512,2,3,128]{4,1,3,2,0:T(8,128)(2,1)}) %all-gather.2.cloned.1.call-update) | async-done | bytes 18874384 | tf_op jit(solution)/shard_map/all_gather | solution.py:48
  168.4 585.6 %while.15 = (s32[]{:T(128)}, f32[8,24,64,2,3]{2,1,4,3,0:T(8,128)}, f32[8,24,64,2,3]{2,1,4,3,0:T(8,128)}, f32[8,24,64,2,3,128]{5,2,4,3,1,0:T(8,128)}, s32[8]{0:T(...) while((s32[]{:T(128)}, f32[8,24,64,2,3]{2,1,4,3,0:T(8,128)}, ...), condition=%wide.region_8.9_spmd.clone, body=%wide.region_3.8_spmd.clone.sunk | while | flops 5245315072 | bytes 178591088 | solution.py:70
  170.0 18.3 %bitcast_reduce_fusion.4 = (f32[24,64,2,3]{1,3,2,0:T(4,128)S(1)}, f32[24,2,64,3,1024]{4,2,3,1,0:T(8,128)}) fusion(pred[24,1024]{1,0:T(8,128)(4,1)S(1)} %compare_bitcast_fusion.2, bf16[24,1024,2,128]{3,1,2,0:T(8,128)(2,1)} %get-tuple-element.331, bf16[24,512,2,3,128]{4,1,3,2,0:T(8,128)(2,1)} %get-tuple-element.330, s32[]{:T(128)S(6)} %select_n.57), kind=kOutput, calls=%fused_computation.3.clone.1 | convolution fusion | flops 2444221440 | bytes 52752388 | tf_op jit(solution)/shard_map/while/body/eval_jaxpr/bqkgd,btkd->bqkgt/dot_general | solution.py:58
  192.1 18.3 %fusion.64 = f32[24,64,2,3]{1,3,2,0:T(4,128)S(1)} fusion(f32[24,2,64,3,1024]{4,2,3,1,0:T(8,128)} %get-tuple-element.285, f32[24,64,2,3]{1,3,2,0:T(4,128)S(1)} %max.22, pred[24,1024]{1,0:T(8,128)(4,1)S(1)} %compare_bitcast_fusion.2), kind=kLoop, calls=%fused_computation.7.clone.1 | loop fusion | flops 37739520 | bytes 37847040 | tf_op jit(solution)/shard_map/while/body/eval_jaxpr/reduce_sum | solution.py:65
  212.7 21.8 %fusion.66 = f32[24,2,64,3,128]{4,2,3,1,0:T(8,128)} fusion(f32[24,2,64,3,1024]{4,2,3,1,0:T(8,128)} %get-tuple-element.285, f32[24,64,2,3]{1,3,2,0:T(4,128)S(1)} %max.22, pred[24,1024]{1,0:T(8,128)(4,1)S(1)} %compare_bitcast_fusion.2, bf16[24,1024,2,128]{3,1,2,0:T(8,128)(2,1)} %get-tuple-element.333), kind=kOutput, calls=%fused_computation.8.clone.1 | convolution fusion | flops 2453667840 | bytes 55111680 | tf_op jit(solution)/shard_map/while/body/eval_jaxpr/bqkgt,btkd->bqkgd/dot_general | solution.py:66
  234.4 7.3 bitcast_dynamic-update-slice_fusion.2
  243.1 18.3 %bitcast_reduce_fusion.4 = (f32[24,64,2,3]{1,3,2,0:T(4,128)S(1)}, f32[24,2,64,3,1024]{4,2,3,1,0:T(8,128)}) fusion(pred[24,1024]{1,0:T(8,128)(4,1)S(1)} %compare_bitcast_fusion.2, bf16[24,1024,2,128]{3,1,2,0:T(8,128)(2,1)} %get-tuple-element.331, bf16[24,512,2,3,128]{4,1,3,2,0:T(8,128)(2,1)} %get-tuple-element.330, s32[]{:T(128)S(6)} %select_n.57), kind=kOutput, calls=%fused_computation.3.clone.1 | convolution fusion | flops 2444221440 | bytes 52752388 | tf_op jit(solution)/shard_map/while/body/eval_jaxpr/bqkgd,btkd->bqkgt/dot_general | solution.py:58
  265.2 18.3 %fusion.64 = f32[24,64,2,3]{1,3,2,0:T(4,128)S(1)} fusion(f32[24,2,64,3,1024]{4,2,3,1,0:T(8,128)} %get-tuple-element.285, f32[24,64,2,3]{1,3,2,0:T(4,128)S(1)} %max.22, pred[24,1024]{1,0:T(8,128)(4,1)S(1)} %compare_bitcast_fusion.2), kind=kLoop, calls=%fused_computation.7.clone.1 | loop fusion | flops 37739520 | bytes 37847040 | tf_op jit(solution)/shard_map/while/body/eval_jaxpr/reduce_sum | solution.py:65
  285.8 21.8 %fusion.66 = f32[24,2,64,3,128]{4,2,3,1,0:T(8,128)} fusion(f32[24,2,64,3,1024]{4,2,3,1,0:T(8,128)} %get-tuple-element.285, f32[24,64,2,3]{1,3,2,0:T(4,128)S(1)} %max.22, pred[24,1024]{1,0:T(8,128)(4,1)S(1)} %compare_bitcast_fusion.2, bf16[24,1024,2,128]{3,1,2,0:T(8,128)(2,1)} %get-tuple-element.333), kind=kOutput, calls=%fused_computation.8.clone.1 | convolution fusion | flops 2453667840 | bytes 55111680 | tf_op jit(solution)/shard_map/while/body/eval_jaxpr/bqkgt,btkd->bqkgd/dot_general | solution.py:66
  307.6 7.3 bitcast_dynamic-update-slice_fusion.2
  316.3 18.3 %bitcast_reduce_fusion.4 = (f32[24,64,2,3]{1,3,2,0:T(4,128)S(1)}, f32[24,2,64,3,1024]{4,2,3,1,0:T(8,128)}) fusion(pred[24,1024]{1,0:T(8,128)(4,1)S(1)} %compare_bitcast_fusion.2, bf16[24,1024,2,128]{3,1,2,0:T(8,128)(2,1)} %get-tuple-element.331, bf16[24,512,2,3,128]{4,1,3,2,0:T(8,128)(2,1)} %get-tuple-element.330, s32[]{:T(128)S(6)} %select_n.57), kind=kOutput, calls=%fused_computation.3.clone.1 | convolution fusion | flops 2444221440 | bytes 52752388 | tf_op jit(solution)/shard_map/while/body/eval_jaxpr/bqkgd,btkd->bqkgt/dot_general | solution.py:58
  338.4 18.3 %fusion.64 = f32[24,64,2,3]{1,3,2,0:T(4,128)S(1)} fusion(f32[24,2,64,3,1024]{4,2,3,1,0:T(8,128)} %get-tuple-element.285, f32[24,64,2,3]{1,3,2,0:T(4,128)S(1)} %max.22, pred[24,1024]{1,0:T(8,128)(4,1)S(1)} %compare_bitcast_fusion.2), kind=kLoop, calls=%fused_computation.7.clone.1 | loop fusion | flops 37739520 | bytes 37847040 | tf_op jit(solution)/shard_map/while/body/eval_jaxpr/reduce_sum | solution.py:65
  359.0 21.8 %fusion.66 = f32[24,2,64,3,128]{4,2,3,1,0:T(8,128)} fusion(f32[24,2,64,3,1024]{4,2,3,1,0:T(8,128)} %get-tuple-element.285, f32[24,64,2,3]{1,3,2,0:T(4,128)S(1)} %max.22, pred[24,1024]{1,0:T(8,128)(4,1)S(1)} %compare_bitcast_fusion.2, bf16[24,1024,2,128]{3,1,2,0:T(8,128)(2,1)} %get-tuple-element.333), kind=kOutput, calls=%fused_computation.8.clone.1 | convolution fusion | flops 2453667840 | bytes 55111680 | tf_op jit(solution)/shard_map/while/body/eval_jaxpr/bqkgt,btkd->bqkgd/dot_general | solution.py:66
  380.7 7.4 bitcast_dynamic-update-slice_fusion.2
  389.5 18.3 %bitcast_reduce_fusion.4 = (f32[24,64,2,3]{1,3,2,0:T(4,128)S(1)}, f32[24,2,64,3,1024]{4,2,3,1,0:T(8,128)}) fusion(pred[24,1024]{1,0:T(8,128)(4,1)S(1)} %compare_bitcast_fusion.2, bf16[24,1024,2,128]{3,1,2,0:T(8,128)(2,1)} %get-tuple-element.331, bf16[24,512,2,3,128]{4,1,3,2,0:T(8,128)(2,1)} %get-tuple-element.330, s32[]{:T(128)S(6)} %select_n.57), kind=kOutput, calls=%fused_computation.3.clone.1 | convolution fusion | flops 2444221440 | bytes 52752388 | tf_op jit(solution)/shard_map/while/body/eval_jaxpr/bqkgd,btkd->bqkgt/dot_general | solution.py:58
  411.6 18.3 %fusion.64 = f32[24,64,2,3]{1,3,2,0:T(4,128)S(1)} fusion(f32[24,2,64,3,1024]{4,2,3,1,0:T(8,128)} %get-tuple-element.285, f32[24,64,2,3]{1,3,2,0:T(4,128)S(1)} %max.22, pred[24,1024]{1,0:T(8,128)(4,1)S(1)} %compare_bitcast_fusion.2), kind=kLoop, calls=%fused_computation.7.clone.1 | loop fusion | flops 37739520 | bytes 37847040 | tf_op jit(solution)/shard_map/while/body/eval_jaxpr/reduce_sum | solution.py:65
  432.2 21.8 %fusion.66 = f32[24,2,64,3,128]{4,2,3,1,0:T(8,128)} fusion(f32[24,2,64,3,1024]{4,2,3,1,0:T(8,128)} %get-tuple-element.285, f32[24,64,2,3]{1,3,2,0:T(4,128)S(1)} %max.22, pred[24,1024]{1,0:T(8,128)(4,1)S(1)} %compare_bitcast_fusion.2, bf16[24,1024,2,128]{3,1,2,0:T(8,128)(2,1)} %get-tuple-element.333), kind=kOutput, calls=%fused_computation.8.clone.1 | convolution fusion | flops 2453667840 | bytes 55111680 | tf_op jit(solution)/shard_map/while/body/eval_jaxpr/bqkgt,btkd->bqkgd/dot_general | solution.py:66
  454.0 7.3 bitcast_dynamic-update-slice_fusion.2
  462.6 18.3 %bitcast_reduce_fusion.4 = (f32[24,64,2,3]{1,3,2,0:T(4,128)S(1)}, f32[24,2,64,3,1024]{4,2,3,1,0:T(8,128)}) fusion(pred[24,1024]{1,0:T(8,128)(4,1)S(1)} %compare_bitcast_fusion.2, bf16[24,1024,2,128]{3,1,2,0:T(8,128)(2,1)} %get-tuple-element.331, bf16[24,512,2,3,128]{4,1,3,2,0:T(8,128)(2,1)} %get-tuple-element.330, s32[]{:T(128)S(6)} %select_n.57), kind=kOutput, calls=%fused_computation.3.clone.1 | convolution fusion | flops 2444221440 | bytes 52752388 | tf_op jit(solution)/shard_map/while/body/eval_jaxpr/bqkgd,btkd->bqkgt/dot_general | solution.py:58
  484.8 18.3 %fusion.64 = f32[24,64,2,3]{1,3,2,0:T(4,128)S(1)} fusion(f32[24,2,64,3,1024]{4,2,3,1,0:T(8,128)} %get-tuple-element.285, f32[24,64,2,3]{1,3,2,0:T(4,128)S(1)} %max.22, pred[24,1024]{1,0:T(8,128)(4,1)S(1)} %compare_bitcast_fusion.2), kind=kLoop, calls=%fused_computation.7.clone.1 | loop fusion | flops 37739520 | bytes 37847040 | tf_op jit(solution)/shard_map/while/body/eval_jaxpr/reduce_sum | solution.py:65
  505.3 21.8 %fusion.66 = f32[24,2,64,3,128]{4,2,3,1,0:T(8,128)} fusion(f32[24,2,64,3,1024]{4,2,3,1,0:T(8,128)} %get-tuple-element.285, f32[24,64,2,3]{1,3,2,0:T(4,128)S(1)} %max.22, pred[24,1024]{1,0:T(8,128)(4,1)S(1)} %compare_bitcast_fusion.2, bf16[24,1024,2,128]{3,1,2,0:T(8,128)(2,1)} %get-tuple-element.333), kind=kOutput, calls=%fused_computation.8.clone.1 | convolution fusion | flops 2453667840 | bytes 55111680 | tf_op jit(solution)/shard_map/while/body/eval_jaxpr/bqkgt,btkd->bqkgd/dot_general | solution.py:66
  527.1 7.3 bitcast_dynamic-update-slice_fusion.2
  535.8 18.3 %bitcast_reduce_fusion.4 = (f32[24,64,2,3]{1,3,2,0:T(4,128)S(1)}, f32[24,2,64,3,1024]{4,2,3,1,0:T(8,128)}) fusion(pred[24,1024]{1,0:T(8,128)(4,1)S(1)} %compare_bitcast_fusion.2, bf16[24,1024,2,128]{3,1,2,0:T(8,128)(2,1)} %get-tuple-element.331, bf16[24,512,2,3,128]{4,1,3,2,0:T(8,128)(2,1)} %get-tuple-element.330, s32[]{:T(128)S(6)} %select_n.57), kind=kOutput, calls=%fused_computation.3.clone.1 | convolution fusion | flops 2444221440 | bytes 52752388 | tf_op jit(solution)/shard_map/while/body/eval_jaxpr/bqkgd,btkd->bqkgt/dot_general | solution.py:58
  557.9 18.3 %fusion.64 = f32[24,64,2,3]{1,3,2,0:T(4,128)S(1)} fusion(f32[24,2,64,3,1024]{4,2,3,1,0:T(8,128)} %get-tuple-element.285, f32[24,64,2,3]{1,3,2,0:T(4,128)S(1)} %max.22, pred[24,1024]{1,0:T(8,128)(4,1)S(1)} %compare_bitcast_fusion.2), kind=kLoop, calls=%fused_computation.7.clone.1 | loop fusion | flops 37739520 | bytes 37847040 | tf_op jit(solution)/shard_map/while/body/eval_jaxpr/reduce_sum | solution.py:65
  578.5 21.8 %fusion.66 = f32[24,2,64,3,128]{4,2,3,1,0:T(8,128)} fusion(f32[24,2,64,3,1024]{4,2,3,1,0:T(8,128)} %get-tuple-element.285, f32[24,64,2,3]{1,3,2,0:T(4,128)S(1)} %max.22, pred[24,1024]{1,0:T(8,128)(4,1)S(1)} %compare_bitcast_fusion.2, bf16[24,1024,2,128]{3,1,2,0:T(8,128)(2,1)} %get-tuple-element.333), kind=kOutput, calls=%fused_computation.8.clone.1 | convolution fusion | flops 2453667840 | bytes 55111680 | tf_op jit(solution)/shard_map/while/body/eval_jaxpr/bqkgt,btkd->bqkgd/dot_general | solution.py:66
  600.3 7.4 bitcast_dynamic-update-slice_fusion.2
  609.0 18.3 %bitcast_reduce_fusion.4 = (f32[24,64,2,3]{1,3,2,0:T(4,128)S(1)}, f32[24,2,64,3,1024]{4,2,3,1,0:T(8,128)}) fusion(pred[24,1024]{1,0:T(8,128)(4,1)S(1)} %compare_bitcast_fusion.2, bf16[24,1024,2,128]{3,1,2,0:T(8,128)(2,1)} %get-tuple-element.331, bf16[24,512,2,3,128]{4,1,3,2,0:T(8,128)(2,1)} %get-tuple-element.330, s32[]{:T(128)S(6)} %select_n.57), kind=kOutput, calls=%fused_computation.3.clone.1 | convolution fusion | flops 2444221440 | bytes 52752388 | tf_op jit(solution)/shard_map/while/body/eval_jaxpr/bqkgd,btkd->bqkgt/dot_general | solution.py:58
  631.2 18.3 %fusion.64 = f32[24,64,2,3]{1,3,2,0:T(4,128)S(1)} fusion(f32[24,2,64,3,1024]{4,2,3,1,0:T(8,128)} %get-tuple-element.285, f32[24,64,2,3]{1,3,2,0:T(4,128)S(1)} %max.22, pred[24,1024]{1,0:T(8,128)(4,1)S(1)} %compare_bitcast_fusion.2), kind=kLoop, calls=%fused_computation.7.clone.1 | loop fusion | flops 37739520 | bytes 37847040 | tf_op jit(solution)/shard_map/while/body/eval_jaxpr/reduce_sum | solution.py:65
  651.7 21.8 %fusion.66 = f32[24,2,64,3,128]{4,2,3,1,0:T(8,128)} fusion(f32[24,2,64,3,1024]{4,2,3,1,0:T(8,128)} %get-tuple-element.285, f32[24,64,2,3]{1,3,2,0:T(4,128)S(1)} %max.22, pred[24,1024]{1,0:T(8,128)(4,1)S(1)} %compare_bitcast_fusion.2, bf16[24,1024,2,128]{3,1,2,0:T(8,128)(2,1)} %get-tuple-element.333), kind=kOutput, calls=%fused_computation.8.clone.1 | convolution fusion | flops 2453667840 | bytes 55111680 | tf_op jit(solution)/shard_map/while/body/eval_jaxpr/bqkgt,btkd->bqkgd/dot_general | solution.py:66
  673.5 7.3 bitcast_dynamic-update-slice_fusion.2
  682.2 18.3 %bitcast_reduce_fusion.4 = (f32[24,64,2,3]{1,3,2,0:T(4,128)S(1)}, f32[24,2,64,3,1024]{4,2,3,1,0:T(8,128)}) fusion(pred[24,1024]{1,0:T(8,128)(4,1)S(1)} %compare_bitcast_fusion.2, bf16[24,1024,2,128]{3,1,2,0:T(8,128)(2,1)} %get-tuple-element.331, bf16[24,512,2,3,128]{4,1,3,2,0:T(8,128)(2,1)} %get-tuple-element.330, s32[]{:T(128)S(6)} %select_n.57), kind=kOutput, calls=%fused_computation.3.clone.1 | convolution fusion | flops 2444221440 | bytes 52752388 | tf_op jit(solution)/shard_map/while/body/eval_jaxpr/bqkgd,btkd->bqkgt/dot_general | solution.py:58
  704.3 18.3 %fusion.64 = f32[24,64,2,3]{1,3,2,0:T(4,128)S(1)} fusion(f32[24,2,64,3,1024]{4,2,3,1,0:T(8,128)} %get-tuple-element.285, f32[24,64,2,3]{1,3,2,0:T(4,128)S(1)} %max.22, pred[24,1024]{1,0:T(8,128)(4,1)S(1)} %compare_bitcast_fusion.2), kind=kLoop, calls=%fused_computation.7.clone.1 | loop fusion | flops 37739520 | bytes 37847040 | tf_op jit(solution)/shard_map/while/body/eval_jaxpr/reduce_sum | solution.py:65
  724.9 21.8 %fusion.66 = f32[24,2,64,3,128]{4,2,3,1,0:T(8,128)} fusion(f32[24,2,64,3,1024]{4,2,3,1,0:T(8,128)} %get-tuple-element.285, f32[24,64,2,3]{1,3,2,0:T(4,128)S(1)} %max.22, pred[24,1024]{1,0:T(8,128)(4,1)S(1)} %compare_bitcast_fusion.2, bf16[24,1024,2,128]{3,1,2,0:T(8,128)(2,1)} %get-tuple-element.333), kind=kOutput, calls=%fused_computation.8.clone.1 | convolution fusion | flops 2453667840 | bytes 55111680 | tf_op jit(solution)/shard_map/while/body/eval_jaxpr/bqkgt,btkd->bqkgd/dot_general | solution.py:66
  746.7 7.4 bitcast_dynamic-update-slice_fusion.2
  754.2 54.5 %all-reduce.3.cloned.1.call-done = f32[8,24,64,2,3]{2,1,4,3,0:T(8,128)} async-done(((f32[8,24,64,2,3]{2,1,4,3,0:T(8,128)}), f32[8,24,64,2,3]{2,1,4,3,0:T(8,128)}) %all-reduce.3.cloned.1.call-update) | async-done | bytes 294928 | tf_op jit(solution)/shard_map/pmax | solution.py:71
  811.4 26.1 %broadcast_multiply_fusion = f32[8,24,64,2,3,128]{5,2,4,3,1,0:T(8,128)} fusion(f32[8,24,64,2,3,128]{5,2,4,3,1,0:T(8,128)} %get-tuple-element.67, f32[8,24,64,2,3]{2,4,3,1,0:T(4,128)S(1)} %copy.71), kind=kLoop, calls=%fused_computation.49 | loop fusion | flops 9437184 | bytes 75792384 | tf_op jit(solution)/shard_map/mul | solution.py:74
  846.3 8.2 div.45
  854.5 175.5 %reduce-scatter.3.cloned.1.call-done = f32[1,24,64,2,3,128]{5,2,4,3,1,0:T(8,128)} async-done(((f32[8,24,64,2,3,128]{5,2,4,3,1,0:T(8,128)}), f32[1,24,64,2,3,128]{5,2,4,3,1,0:T(8,128)}) %reduce-scatter.3.cloned.1.call-update) | async-done | bytes 4718608 | tf_op jit(solution)/shard_map/reduce_scatter | solution.py:74
  1030.0 8.5 copy.72
  1038.5 8.3 reduce_scatter.18
  1046.8 15.1 %fusion.38 = f32[1536,3072]{1,0:T(8,128)} fusion(bf16[768,3072]{1,0:T(8,128)(2,1)} %param.17, f32[1536,768]{1,0:T(8,128)} %reduce_scatter.18, f32[1536,768]{1,0:T(8,128)} %div.45), kind=kOutput, calls=%fused_computation.56 | convolution fusion | flops 7250116608 | bytes 33030144 | tf_op jit(solution)/shard_map/dot_general | solution.py:76
  1062.6 323.2 %all-reduce.5.cloned.1.call-done = f32[1536,3072]{1,0:T(8,128)} async-done(((f32[1536,3072]{1,0:T(8,128)}), f32[1536,3072]{1,0:T(8,128)}) %all-reduce.5.cloned.1.call-update) | async-done | bytes 18874384 | tf_op jit(solution)/shard_map/psum | solution.py:77
  1385.8 7.7 multiply_reduce_fusion
  1393.6 9.2 multiply_multiply_fusion
  (180 shorter events, 119.6 us)
Async XLA Ops:
  7.2 14.1 copy-start
  7.2 161.2 %all-gather.2.cloned.1.call-start = ((), (), s32[]{:S(2)}) async-start(), calls=%async_computation.2 | async-start | bytes 21233664 | tf_op jit(solution)/shard_map/all_gather | solution.py:48
  8.1 13.2 copy-start.3
  52.7 6.6 copy-start.7
  73.3 735.4 %all-reduce.3.cloned.1.call-start = ((), (), s32[]{:S(2)}) async-start(), calls=%async_computation.3 | async-start | bytes 1179648 | tf_op jit(solution)/shard_map/pmax | solution.py:71
  73.5 11.6 copy-start.10
  73.6 11.6 copy-start.6
  91.3 14.7 %slice-start = ((s8[9437184]{0:T(1024)(128)(4,1)}), s8[4194304]{0:T(1024)(128)(4,1)S(1)}, s32[]{:S(2)}) async-start(s8[9437184]{0:T(1024)(128)(4,1)} %bitcast.104), calls=%async_computation.7 | async-start | bytes 8388608
  93.5 12.6 copy-start.5
  93.7 12.4 slice-start.1
  93.7 12.4 slice-start.2
  93.7 12.4 copy-start.9
  108.9 59.5 %copy-start.4 = (bf16[24,64,2,128]{3,2,1,0:T(2,128)(2,1)}, bf16[24,64,2,128]{3,2,1,0:T(2,128)(2,1)S(1)}, u32[]{:S(2)}) copy-start(bf16[24,64,2,128]{3,2,1,0:T(2,128)(2,1)S(1)} %reshape.205) | copy-start | bytes 2359300
  192.0 18.3 %copy-start.2 = (f32[24,2,64,3,64]{2,4,3,1,0:T(8,128)}, f32[24,2,64,3,64]{2,4,3,1,0:T(8,128)S(1)}, u32[]{:S(2)}) copy-start(f32[24,2,64,3,64]{2,4,3,1,0:T(8,128)S(1)} %get-tuple-element.288) | copy-start | bytes 7077892 | tf_op jit(solution)/shard_map/while
  265.2 18.3 %copy-start.2 = (f32[24,2,64,3,64]{2,4,3,1,0:T(8,128)}, f32[24,2,64,3,64]{2,4,3,1,0:T(8,128)S(1)}, u32[]{:S(2)}) copy-start(f32[24,2,64,3,64]{2,4,3,1,0:T(8,128)S(1)} %get-tuple-element.288) | copy-start | bytes 7077892 | tf_op jit(solution)/shard_map/while
  338.3 18.3 %copy-start.2 = (f32[24,2,64,3,64]{2,4,3,1,0:T(8,128)}, f32[24,2,64,3,64]{2,4,3,1,0:T(8,128)S(1)}, u32[]{:S(2)}) copy-start(f32[24,2,64,3,64]{2,4,3,1,0:T(8,128)S(1)} %get-tuple-element.288) | copy-start | bytes 7077892 | tf_op jit(solution)/shard_map/while
  411.6 18.3 %copy-start.2 = (f32[24,2,64,3,64]{2,4,3,1,0:T(8,128)}, f32[24,2,64,3,64]{2,4,3,1,0:T(8,128)S(1)}, u32[]{:S(2)}) copy-start(f32[24,2,64,3,64]{2,4,3,1,0:T(8,128)S(1)} %get-tuple-element.288) | copy-start | bytes 7077892 | tf_op jit(solution)/shard_map/while
  484.7 18.3 %copy-start.2 = (f32[24,2,64,3,64]{2,4,3,1,0:T(8,128)}, f32[24,2,64,3,64]{2,4,3,1,0:T(8,128)S(1)}, u32[]{:S(2)}) copy-start(f32[24,2,64,3,64]{2,4,3,1,0:T(8,128)S(1)} %get-tuple-element.288) | copy-start | bytes 7077892 | tf_op jit(solution)/shard_map/while
  557.9 18.3 %copy-start.2 = (f32[24,2,64,3,64]{2,4,3,1,0:T(8,128)}, f32[24,2,64,3,64]{2,4,3,1,0:T(8,128)S(1)}, u32[]{:S(2)}) copy-start(f32[24,2,64,3,64]{2,4,3,1,0:T(8,128)S(1)} %get-tuple-element.288) | copy-start | bytes 7077892 | tf_op jit(solution)/shard_map/while
  631.1 18.3 %copy-start.2 = (f32[24,2,64,3,64]{2,4,3,1,0:T(8,128)}, f32[24,2,64,3,64]{2,4,3,1,0:T(8,128)S(1)}, u32[]{:S(2)}) copy-start(f32[24,2,64,3,64]{2,4,3,1,0:T(8,128)S(1)} %get-tuple-element.288) | copy-start | bytes 7077892 | tf_op jit(solution)/shard_map/while
  704.3 18.3 %copy-start.2 = (f32[24,2,64,3,64]{2,4,3,1,0:T(8,128)}, f32[24,2,64,3,64]{2,4,3,1,0:T(8,128)S(1)}, u32[]{:S(2)}) copy-start(f32[24,2,64,3,64]{2,4,3,1,0:T(8,128)S(1)} %get-tuple-element.288) | copy-start | bytes 7077892 | tf_op jit(solution)/shard_map/while
  754.1 84.8 %reduce-scatter.5.cloned.1.call-start = ((), (), s32[]{:S(2)}) async-start(), calls=%async_computation.5 | async-start | bytes 663552 | tf_op jit(solution)/shard_map/reduce_scatter | solution.py:73
  811.3 218.7 %reduce-scatter.3.cloned.1.call-start = ((), (), s32[]{:S(2)}) async-start(), calls=%async_computation.4 | async-start | bytes 42467328 | tf_op jit(solution)/shard_map/reduce_scatter | solution.py:74
  837.5 548.3 %all-reduce.5.cloned.1.call-start = ((), (), s32[]{:S(2)}) async-start(), calls=%async_computation.6 | async-start | bytes 37748736 | tf_op jit(solution)/shard_map/psum | solution.py:77
  1061.9 0.7 copy-start.8
  1385.8 17.1 %slice-start.3 = ((s8[9437184]{0:T(1024)(128)(4,1)}), s8[1048576]{0:T(1024)(128)(4,1)S(1)}, s32[]{:S(2)}) async-start(s8[9437184]{0:T(1024)(128)(4,1)} %bitcast.107), calls=%async_computation.10 | async-start | bytes 2097152
  1393.5 9.3 slice-start.4
  1393.6 9.3 slice-start.5
  1402.9 5.4 copy-start.1
Sparse Core Ops, SparseCore 0:
  73.4 94.9 all-gather.1
  754.2 54.3 all-reduce.2
  811.5 27.2 reduce-scatter.4
  841.1 188.8 reduce-scatter.2
  1062.1 323.6 all-reduce.4
where the time goes:
time: 1420 us
  waiting for transfers between devices  614 us (43%)
  matrix products  444 us (31%)
  other arithmetic  234 us (16%)
  local copies, waits for them, and re-layouts  85.7 us (6%)
  blocking collectives  16.5 us (1%)
  between operations  14.6 us (1%)
    psum x1, waiting for transfers between devices, local_step(): mixed_sum = lax.psum(mixed_part, 'tp')  323 us
    reduce_scatter x1, waiting for transfers between devices, local_step(): lax.psum_scatter(part_num * factor[..., None], 'cp', scatter_dimension=0,...  175 us
    dot_general x8, matrix products, block_attention(): jnp.einsum('bqkgt,btkd->bqkgd', p_cache.astype(jnp.bfloat16), cache_v, pr...  174 us
    reduce_sum x16, other arithmetic, block_attention(): den_sum = jnp.sum(p_cache, axis=-1) + jnp.sum(p_chunk, axis=-1)  159 us
    dot_general x8, matrix products, block_attention(): jnp.einsum('bqkgd,btkd->bqkgt', q_blk, cache_k, preferred_element_type=jn...  147 us
    all_gather x1, waiting for transfers between devices, local_step(): q_all = lax.all_gather(q_new, 'cp', axis=1, tiled=True)  59.3 us
    dot_general x8, matrix products, block_attention(): jnp.einsum('bqkgt,btkd->bqkgd', p_chunk.astype(jnp.bfloat16), chunk_v, pr...  58.8 us
    pmax x1, waiting for transfers between devices, local_step(): glob_max = lax.pmax(part_max, 'cp')  54.5 us
  transfers between devices with their start and end apart: 5, of which 5 were waited for; matrix products, arithmetic and copies ran while one was open for 5% of the time, Pallas kernels for 0%

commit v1 on v0

v1 whole, which is shorter than its diff:
```python
import functools
import math

import jax
import jax.numpy as jnp
from jax import lax
from jax.experimental import pallas as pl
from jax.experimental.pallas import tpu as pltpu
from jax.sharding import PartitionSpec as P

NORM_EPS = 1e-6
ROPE_BASE = 500000.0
MASK_VALUE = -1e30
ROW_CHUNKS = 3
QUERY_TILE = 256
TOKEN_TILE = 256
KEY_PIECE = 512
VMEM_BYTES = 60 * 1024 * 1024
MESH = pl.DeviceIdType.MESH


def rope_tables(positions, head_dim):
    half_dim = head_dim // 2
    inv_freq = ROPE_BASE ** (-(jnp.arange(half_dim, dtype=jnp.float32) * 2.0 / head_dim))
    angles = positions.astype(jnp.float32)[:, None] * inv_freq
    cos_tab, sin_tab = jnp.cos(angles), jnp.sin(angles)
    return jnp.concatenate([cos_tab, cos_tab], axis=-1), jnp.concatenate([-sin_tab, sin_tab], axis=-1)


def exchange_kernel(axis, size, combine, x_ref, out_ref, held, send_sem, recv_sem):
    me = lax.axis_index(axis)
    barrier = pltpu.get_barrier_semaphore()
    for step in range(1, size):
        pl.semaphore_signal(barrier, inc=1, device_id={axis: lax.rem(me + step, size)}, device_id_type=MESH)
    pl.semaphore_wait(barrier, size - 1)
    copies = []
    for step in range(1, size):
        copy = pltpu.make_async_remote_copy(
            src_ref=x_ref,
            dst_ref=held.at[me],
            send_sem=send_sem.at[step - 1],
            recv_sem=recv_sem.at[step - 1],
            device_id={axis: lax.rem(me + step, size)},
            device_id_type=MESH,
        )
        copy.start()
        copies.append(copy)
    held[me] = x_ref[...]
    for copy in copies:
        copy.wait()
    if combine == 'sum':
        total = held[0]
        for src in range(1, size):
            total = total + held[src]
        out_ref[...] = total
    else:
        top = held[0]
        for src in range(1, size):
            top = jnp.maximum(top, held[src])
        total = jnp.exp2(held[0] - top)
        for src in range(1, size):
            total = total + jnp.exp2(held[src] - top)
        out_ref[...] = top + jnp.log2(total)


def exchange(vals, axis, size, combine, collective_id):
    return pl.pallas_call(
        functools.partial(exchange_kernel, axis, size, combine),
        out_shape=jax.ShapeDtypeStruct(vals.shape, vals.dtype),
        in_specs=[pl.BlockSpec(memory_space=pltpu.VMEM)],
        out_specs=pl.BlockSpec(memory_space=pltpu.VMEM),
        scratch_shapes=[
            pltpu.VMEM((size,) + vals.shape, vals.dtype),
            pltpu.SemaphoreType.DMA((size - 1,)),
            pltpu.SemaphoreType.DMA((size - 1,)),
        ],
        compiler_params=pltpu.CompilerParams(collective_id=collective_id, has_side_effects=True),
        cost_estimate=pl.CostEstimate(flops=8_000_000, bytes_accessed=2 * vals.size * 4, transcendentals=0),
        name='exchange_' + axis,
    )(vals)


def rope_kernel(head_dim, q_ref, k_ref, q_inv, k_inv, q_gain, k_gain, cos_ref, sin_ref, q_out, k_out):
    cos_tab, sin_tab = cos_ref[...], sin_ref[...]
    for raw, inv, gain, out in ((q_ref, q_inv, q_gain, q_out), (k_ref, k_inv, k_gain, k_out)):
        scale = inv[...]
        for head in range(raw.shape[1] // head_dim):
            cols = slice(head * head_dim, (head + 1) * head_dim)
            vals = raw[:, cols] * scale * gain[:, cols]
            out[:, cols] = (vals * cos_tab + pltpu.roll(vals, head_dim // 2, 1) * sin_tab).astype(out.dtype)


def norm_rope(q_raw, k_raw, q_inv, k_inv, q_gain, k_gain, cos_tab, sin_tab, head_dim):
    tokens, q_width = q_raw.shape
    k_width = k_raw.shape[1]
    tile = math.gcd(tokens, TOKEN_TILE)
    by_token = lambda width: pl.BlockSpec((tile, width), lambda i: (i, 0))
    whole = lambda width: pl.BlockSpec((1, width), lambda i: (0, 0))
    return pl.pallas_call(
        functools.partial(rope_kernel, head_dim),
        grid=(tokens // tile,),
        out_shape=(jax.ShapeDtypeStruct(q_raw.shape, jnp.bfloat16), jax.ShapeDtypeStruct(k_raw.shape, jnp.bfloat16)),
        in_specs=[by_token(q_width), by_token(k_width), by_token(head_dim), by_token(head_dim), whole(q_width), whole(k_width), by_token(head_dim), by_token(head_dim)],
        out_specs=(by_token(q_width), by_token(k_width)),
        compiler_params=pltpu.CompilerParams(vmem_limit_bytes=VMEM_BYTES),
        cost_estimate=pl.CostEstimate(flops=tokens * q_width * 8, bytes_accessed=tokens * (q_width + k_width) * 6, transcendentals=0),
        name='norm_rope',
    )(q_raw, k_raw, q_inv, k_inv, q_gain, k_gain, cos_tab, sin_tab)


def attention_kernel(row0, groups, exp_scale, info, q_ref, k_ref, v_ref, kc_ref, vc_ref, num_ref, max_ref, lse_ref, vt_ref, s_even, s_odd):
    blocks, _, chunk_dev, _ = q_ref.shape
    cache_dev, head_dim = k_ref.shape[2], k_ref.shape[3]
    per_tile = QUERY_TILE // chunk_dev
    halves = blocks // per_tile
    valid = info[1 + row0 + pl.program_id(0)]
    key_base = info[0]
    tiles = groups * halves
    piece = math.gcd(cache_dev, KEY_PIECE)
    scratch = (s_even, s_odd)

    def q_tile(tile):
        group, half = divmod(tile, halves)
        block = q_ref[half * per_tile:(half + 1) * per_tile, 0, :, group * head_dim:(group + 1) * head_dim]
        return block.reshape(QUERY_TILE, head_dim)

    def scores(keys, q_vals):
        return lax.dot_general(keys, q_vals, (((1,), (1,)), ((), ())), preferred_element_type=jnp.float32)

    def fold(vals):
        return jnp.max(vals.reshape(vals.shape[0] // 8, 8, QUERY_TILE), axis=0)

    def chunk_scores(tile, q_vals):
        vals = scores(kc_ref[0], q_vals)
        key_index = key_base + lax.broadcasted_iota(jnp.int32, vals.shape, 0)
        query_index = (tile % halves) * QUERY_TILE + lax.broadcasted_iota(jnp.int32, vals.shape, 1)
        vals = jnp.where(key_index <= query_index, vals, MASK_VALUE)
        scratch[tile % 2][cache_dev:cache_dev + chunk_dev, :] = vals
        return fold(vals)

    def cache_scores(tile, q_vals, first, masked):
        vals = scores(k_ref[0, 0, first:first + piece, :], q_vals)
        if masked:
            slot = first + lax.broadcasted_iota(jnp.int32, vals.shape, 0)
            vals = jnp.where(slot < valid, vals, MASK_VALUE)
        scratch[tile % 2][first:first + piece, :] = vals
        return fold(vals)

    def weights(tile, first, size, top_scaled):
        probs = jnp.exp2(scratch[tile % 2][first:first + size, :] * exp_scale - top_scaled)
        return probs.astype(jnp.bfloat16), jnp.sum(probs.reshape(size // 8, 8, QUERY_TILE), axis=0)

    def run(masked, with_cache):
        firsts = range(0, cache_dev, piece) if with_cache else ()

        def first_scores(tile):
            q_vals = q_tile(tile)
            top = chunk_scores(tile, q_vals)
            for first in firsts:
                top = jnp.maximum(top, cache_scores(tile, q_vals, first, masked))
            return top

        top = first_scores(0)
        for tile in range(tiles):
            top_scaled = jnp.max(top, axis=0, keepdims=True) * exp_scale
            more = tile + 1 < tiles
            if more:
                q_next = q_tile(tile + 1)
                top = chunk_scores(tile + 1, q_next)
            probs, den = weights(tile, cache_dev, chunk_dev, top_scaled)
            num = lax.dot_general(vc_ref[0], probs, (((0,), (0,)), ((), ())), preferred_element_type=jnp.float32)
            for first in firsts:
                if more:
                    top = jnp.maximum(top, cache_scores(tile + 1, q_next, first, masked))
                probs, part = weights(tile, first, piece, top_scaled)
                den = den + part
                num = num + jnp.dot(vt_ref[:, first:first + piece], probs, preferred_element_type=jnp.float32)
            num_ref[0, 0, tile] = num
            max_ref[0, 0, tile:tile + 1, :] = top_scaled
            lse_ref[0, 0, tile:tile + 1, :] = top_scaled + jnp.log2(jnp.sum(den, axis=0, keepdims=True))

    max_ref[...] = jnp.zeros_like(max_ref)
    lse_ref[...] = jnp.zeros_like(lse_ref)

    @pl.when(valid > 0)
    def _():
        vt_ref[...] = v_ref[0, 0].T

    pl.when(valid >= cache_dev)(lambda: run(False, True))
    pl.when(jnp.logical_and(valid > 0, valid < cache_dev))(lambda: run(True, True))
    pl.when(valid <= 0)(lambda: run(False, False))


def attention(info, q_all, k_heads, v_heads, chunk_k, chunk_v, row0, groups):
    blocks, rows, chunk_dev, q_width = q_all.shape
    _, kv_local, cache_dev, head_dim = k_heads.shape
    tiles = groups * (blocks * chunk_dev // QUERY_TILE)
    pad = -(-tiles // 8) * 8
    q_head_width = q_width // kv_local
    stats = jax.ShapeDtypeStruct((rows, kv_local, pad, QUERY_TILE), jnp.float32)
    stats_spec = pl.BlockSpec((1, 1, pad, QUERY_TILE), lambda r, h, _: (r, h, 0, 0))
    scores = rows * q_width // head_dim * blocks * chunk_dev * (cache_dev + chunk_dev)
    return pl.pallas_call(
        functools.partial(attention_kernel, row0, groups, math.log2(math.e) * head_dim ** -0.5),
        out_shape=(jax.ShapeDtypeStruct((rows, kv_local, tiles, head_dim, QUERY_TILE), jnp.float32), stats, stats),
        grid_spec=pltpu.PrefetchScalarGridSpec(
            num_scalar_prefetch=1,
            grid=(rows, kv_local),
            in_specs=[
                pl.BlockSpec((blocks, 1, chunk_dev, q_head_width), lambda r, h, _: (0, r, 0, h)),
                pl.BlockSpec((1, 1, cache_dev, head_dim), lambda r, h, _: (row0 + r, h, 0, 0)),
                pl.BlockSpec((1, 1, cache_dev, head_dim), lambda r, h, _: (row0 + r, h, 0, 0)),
                pl.BlockSpec((1, chunk_dev, head_dim), lambda r, h, _: (row0 + r, 0, h)),
                pl.BlockSpec((1, chunk_dev, head_dim), lambda r, h, _: (row0 + r, 0, h)),
            ],
            out_specs=(pl.BlockSpec((1, 1, tiles, head_dim, QUERY_TILE), lambda r, h, _: (r, h, 0, 0, 0)), stats_spec, stats_spec),
            scratch_shapes=[
                pltpu.VMEM((head_dim, cache_dev), jnp.bfloat16),
                pltpu.VMEM((cache_dev + chunk_dev, QUERY_TILE), jnp.float32),
                pltpu.VMEM((cache_dev + chunk_dev, QUERY_TILE), jnp.float32),
            ],
        ),
        compiler_params=pltpu.CompilerParams(vmem_limit_bytes=VMEM_BYTES),
        cost_estimate=pl.CostEstimate(flops=scores * head_dim * 8, bytes_accessed=scores // 8, transcendentals=scores),
        name='attention',
    )(info, q_all, k_heads, v_heads, chunk_k, chunk_v)


def scale_kernel(num_ref, max_ref, lse_ref, out_ref):
    _, kv_local, tiles, head_dim, _ = num_ref.shape
    blocks, chunk_dev, _ = out_ref.shape
    halves = blocks * chunk_dev // QUERY_TILE
    groups = tiles // halves
    per_tile = QUERY_TILE // chunk_dev
    for kv_head in range(kv_local):
        factor = jnp.exp2(max_ref[0, kv_head] - lse_ref[0, kv_head])
        for group in range(groups):
            head = kv_head * groups + group
            for half in range(halves):
                at = group * halves + half
                scaled = (num_ref[0, kv_head, at] * factor[at:at + 1, :]).T
                out_ref[half * per_tile:(half + 1) * per_tile, :, head * head_dim:(head + 1) * head_dim] = scaled.reshape(per_tile, chunk_dev, head_dim)


def scale_parts(num, tops, lse, blocks, chunk_dev):
    rows, kv_local, tiles, head_dim, _ = num.shape
    pad = tops.shape[2]
    width = kv_local * tiles * QUERY_TILE // (blocks * chunk_dev) * head_dim
    stats_spec = pl.BlockSpec((1, kv_local, pad, QUERY_TILE), lambda r: (r, 0, 0, 0))
    return pl.pallas_call(
        scale_kernel,
        grid=(rows,),
        out_shape=jax.ShapeDtypeStruct((blocks, rows * chunk_dev, width), jnp.float32),
        in_specs=[pl.BlockSpec((1, kv_local, tiles, head_dim, QUERY_TILE), lambda r: (r, 0, 0, 0, 0)), stats_spec, stats_spec],
        out_specs=pl.BlockSpec((blocks, chunk_dev, width), lambda r: (0, r, 0)),
        compiler_params=pltpu.CompilerParams(vmem_limit_bytes=VMEM_BYTES),
        cost_estimate=pl.CostEstimate(flops=num.size * 2, bytes_accessed=num.size * 8, transcendentals=0),
        name='scale_parts',
    )(num, tops, lse)


def out_kernel(tp_size, first, info, *refs):
    o_ref, w_ref, x_ref, gain_ref = refs[:4]
    out_ref = refs[-1]
    me = info[0]
    total = None
    for src in range(tp_size):
        part = jnp.dot(o_ref[lax.rem(src - me + tp_size, tp_size)], w_ref[src], preferred_element_type=jnp.float32)
        total = part if total is None else total + part
    normed = total * lax.rsqrt(jnp.mean(total * total, axis=-1, keepdims=True) + NORM_EPS) * gain_ref[...]
    out_ref[...] = (x_ref[...].astype(jnp.float32) + normed).astype(out_ref.dtype)


def project_out(info, o_all, w_full, x_tokens, gain, earlier, token0):
    tp_size, tokens, width = o_all.shape
    model_dim = x_tokens.shape[1]
    tile = math.gcd(tokens, TOKEN_TILE)
    shift = token0 // tile
    here = lambda i, _: (shift + i, 0)
    in_specs = [
        pl.BlockSpec((tp_size, tile, width), lambda i, _: (0, i, 0)),
        pl.BlockSpec((tp_size, width, model_dim), lambda i, _: (0, 0, 0), pipeline_mode=pl.Buffered(1)),
        pl.BlockSpec((tile, model_dim), here),
        pl.BlockSpec((1, model_dim), lambda i, _: (0, 0)),
    ]
    operands = [info, o_all, w_full, x_tokens, gain]
    aliases = {}
    if earlier is not None:
        in_specs.append(pl.BlockSpec(memory_space=pl.ANY))
        operands.append(earlier)
        aliases = {5: 0}
    return pl.pallas_call(
        functools.partial(out_kernel, tp_size, earlier is None),
        out_shape=jax.ShapeDtypeStruct(x_tokens.shape, jnp.bfloat16),
        grid_spec=pltpu.PrefetchScalarGridSpec(
            num_scalar_prefetch=1,
            grid=(tokens // tile,),
            in_specs=in_specs,
            out_specs=pl.BlockSpec((tile, model_dim), here),
        ),
        input_output_aliases=aliases,
        compiler_params=pltpu.CompilerParams(vmem_limit_bytes=VMEM_BYTES),
        cost_estimate=pl.CostEstimate(flops=2 * tokens * tp_size * width * model_dim, bytes_accessed=2 * w_full.size, transcendentals=0),
        name='project_out',
    )(*operands)


def gather_by_distance(vals, axis, size):
    up = [(i, (i + 1) % size) for i in range(size)]
    down = [(i, (i - 1) % size) for i in range(size)]
    if size != 4:
        steps = [vals]
        for _ in range(size - 1):
            steps.append(lax.ppermute(steps[-1], axis, down))
        return jnp.stack(steps)
    mid = vals.shape[0] // 2
    below = lax.ppermute(vals, axis, up)
    above = lax.ppermute(vals, axis, down)
    far_low = lax.ppermute(below[:mid], axis, up)
    far_high = lax.ppermute(above[mid:], axis, down)
    return jnp.stack([vals, above, jnp.concatenate([far_low, far_high]), below])


def solution(mesh):
    cp_size = mesh.shape['cp']
    tp_size = mesh.shape['tp']

    def local_step(x_chunk, w_query, w_key, w_value, w_out, q_gain, k_gain, post_gain, cache_k, cache_v, prefix_len):
        batch_rows, chunk_dev, model_dim = x_chunk.shape
        cache_dev, kv_local, head_dim = cache_k.shape[1:]
        q_width, k_width = w_query.shape[1], w_key.shape[1]
        groups = q_width // k_width
        cp_index = lax.axis_index('cp')
        tp_index = lax.axis_index('tp')
        rows = batch_rows // ROW_CHUNKS
        tokens = x_chunk.reshape(batch_rows * chunk_dev, model_dim)

        w_piece = w_out.shape[0] // cp_size
        w_own = lax.dynamic_slice_in_dim(w_out, cp_index * w_piece, w_piece, axis=0)
        w_full = lax.all_gather(w_own, ('tp', 'cp'), axis=0, tiled=True).reshape(tp_size, q_width, model_dim)

        q_raw = jnp.dot(tokens, w_query, preferred_element_type=jnp.float32)
        k_raw = jnp.dot(tokens, w_key, preferred_element_type=jnp.float32)
        chunk_v = jnp.dot(tokens, w_value, preferred_element_type=jnp.float32).astype(jnp.bfloat16)
        squares = jnp.stack([jnp.sum(q_raw * q_raw, axis=-1), jnp.sum(k_raw * k_raw, axis=-1)])
        square_sums = exchange(squares.reshape(-1, 128), 'tp', tp_size, 'sum', 0).reshape(squares.shape)
        q_inv = lax.rsqrt(square_sums[0] / (q_width * tp_size) + NORM_EPS)
        k_inv = lax.rsqrt(square_sums[1] / (k_width * tp_size) + NORM_EPS)
        wide = lambda vec: jnp.broadcast_to(vec[:, None], (vec.shape[0], head_dim))
        positions = (prefix_len[:, None] + cp_index * chunk_dev + jnp.arange(chunk_dev, dtype=jnp.int32)[None, :]).reshape(-1)
        cos_tab, sin_tab = rope_tables(positions, head_dim)
        q_new, chunk_k = norm_rope(
            q_raw, k_raw, wide(q_inv), wide(k_inv), q_gain.astype(jnp.float32)[None, :], k_gain.astype(jnp.float32)[None, :], cos_tab, sin_tab, head_dim
        )
        q_new, w_full = lax.optimization_barrier((q_new, w_full))
        q_new = q_new.reshape(batch_rows, chunk_dev, q_width)
        k_rows = chunk_k.reshape(batch_rows, chunk_dev, k_width)
        v_rows = chunk_v.reshape(batch_rows, chunk_dev, k_width)
        k_heads = jnp.transpose(cache_k, (0, 2, 1, 3))
        v_heads = jnp.transpose(cache_v, (0, 2, 1, 3))
        valid = jnp.clip(prefix_len - cp_index * cache_dev, 0, cache_dev)
        info = jnp.concatenate([jnp.reshape(cp_index * chunk_dev, (1,)), valid]).astype(jnp.int32)
        tp_info = jnp.reshape(tp_index, (1,)).astype(jnp.int32)
        post = post_gain.astype(jnp.float32)[None, :]

        gathered = [lax.all_gather(q_new[c * rows:(c + 1) * rows], 'cp', axis=0, tiled=False) for c in range(ROW_CHUNKS)]
        parts = []
        for c in range(ROW_CHUNKS):
            num, tops, lse = attention(info, gathered[c], k_heads, v_heads, k_rows, v_rows, c * rows, groups)
            lse_all = exchange(lse.reshape(-1, QUERY_TILE), 'cp', cp_size, 'lse', 1 + c).reshape(lse.shape)
            scaled = scale_parts(num, tops, lse_all, cp_size, chunk_dev)
            parts.append(lax.psum_scatter(scaled, 'cp', scatter_dimension=0, tiled=False))
        block_out = None
        for c in range(ROW_CHUNKS):
            part = parts[c]
            if c:
                part, block_out = lax.optimization_barrier((part, block_out))
            o_all = gather_by_distance(part.astype(jnp.bfloat16), 'tp', tp_size)
            block_out = project_out(tp_info, o_all, w_full, tokens, post, block_out, c * rows * chunk_dev)
        heads_shape = (batch_rows, chunk_dev, kv_local, head_dim)
        return block_out.reshape(x_chunk.shape), chunk_k.reshape(heads_shape), chunk_v.reshape(heads_shape)

    x_spec = P('dp', 'cp', None)
    head_spec = P('dp', 'cp', 'tp', None)
    in_specs = (x_spec, P(None, 'tp'), P(None, 'tp'), P(None, 'tp'), P('tp', None), P('tp'), P('tp'), P(None), head_spec, head_spec, P('dp'))
    out_specs = (x_spec, head_spec, head_spec)
    return jax.shard_map(local_step, mesh=mesh, in_specs=in_specs, out_specs=out_specs, check_vma=False)
```

time: 1420 us -> 577 us (0.41)
  waiting for transfers between devices: 614 us -> 112 us
  matrix products: 444 us -> 25.5 us
  Pallas kernels: 0 us -> 329 us
  other arithmetic: 234 us -> 20.2 us
  local copies, waits for them, and re-layouts: 85.7 us -> 43.1 us
  starting transfers between devices: 0.49 us -> 22.6 us
  blocking collectives: 16.5 us -> 0 us
    dot_general x34 -> x1, matrix products: 427 us -> 7.19 us  [local_step(): jnp.dot(tokens, w_value, preferred_element_type=jnp.float32)]
    pallas_call x0 -> x14, Pallas kernels: none -> 329 us  [the longest x3 141 us: attention(): pl.pallas_call(functools.partial(attention_kernel, row0, groups, math.log...]
    psum x1 -> x0, waiting for transfers between devices: 323 us -> none  [local_step(): mixed_sum = lax.psum(mixed_part, 'tp')]
    reduce_scatter x2 -> x3, waiting for transfers between devices: 177 us -> 0.02 us  [local_step(): lax.psum_scatter(scaled, 'cp', scatter_dimension=0, tiled=False)]
    reduce_sum x17 -> x0, other arithmetic: 166 us -> none  [the longest x16 159 us: block_attention(): den_sum = jnp.sum(p_cache, axis=-1) + jnp.sum(p_chunk, axis=-1)]
    ppermute x0 -> x12, waiting for transfers between devices: none -> 75.8 us  [the longest x3 49.5 us: gather_by_distance(): above = lax.ppermute(vals, axis, down)]
    pmax x1 -> x0, waiting for transfers between devices: 54.5 us -> none  [local_step(): glob_max = lax.pmax(part_max, 'cp')]
    mul x5 -> x0, other arithmetic: 42.8 us -> none  [the longest x1 26.1 us: local_step(): part_num * factor[..., None]]
  transfers between devices with their start and end apart: 5 -> 19, of which waited for: 5 -> 11; matrix products, arithmetic and copies ran while one was open for 5% -> 14% of each run, Pallas kernels for 0% -> 55%
where the time goes in v1:
time: 577 us; the launch traced here: 567 us
  Pallas kernels  329 us (57%)
  waiting for transfers between devices  112 us (19%)
  local copies, waits for them, and re-layouts  43.1 us (7%)
  matrix products  25.5 us (4%)
  starting transfers between devices  22.6 us (4%)
  other arithmetic  20.2 us (4%)
  between operations  14.9 us (3%)
    pallas_call x3, Pallas kernels, attention(): pl.pallas_call(functools.partial(attention_kernel, row0, groups, math.log...  141 us
    pallas_call x4, Pallas kernels, exchange(): pl.pallas_call(functools.partial(exchange_kernel, axis, size, combine), o...  82.6 us
    pallas_call x3, Pallas kernels, project_out(): pl.pallas_call(functools.partial(out_kernel, tp_size, earlier is None), o...  59.6 us
    ppermute x3, waiting for transfers between devices, gather_by_distance(): above = lax.ppermute(vals, axis, down)  49.5 us
    pallas_call x3, Pallas kernels, scale_parts(): pl.pallas_call(scale_kernel, grid=(rows,), out_shape=jax.ShapeDtypeStruct...  38.4 us
    all_gather x1, waiting for transfers between devices, local_step(): lax.all_gather(w_own, ('tp', 'cp'), axis=0, tiled=True)  25.5 us
    transpose x1, local copies, waits for them, and re-layouts, local_step(): v_heads = jnp.transpose(cache_v, (0, 2, 1, 3))  19.3 us
    ppermute x3, waiting for transfers between devices, gather_by_distance(): far_high = lax.ppermute(above[mid:], axis, down)  14.8 us
  transfers between devices with their start and end apart: 19, of which 11 were waited for; matrix products, arithmetic and copies ran while one was open for 14% of the time, Pallas kernels for 55%

profile of v1, /device:TPU:97, one launch (start us, length us, event | category | flops | bytes accessed | tf_op | source)
XLA Modules:
  0.0 566.9 jit_solution(3573601061235292139)
XLA Ops:
  7.3 2.0 constant_dynamic-slice_fusion
  9.4 13.1 %multiply_reduce_fusion = (f32[1536]{0:T(1024)S(1)}, f32[1536,768]{0,1:T(8,128)}) fusion(bf16[1536,3072]{1,0:T(8,128)(2,1)} %bitcast.55, bf16[3072,768]{1,0:T(8,128)(2,1)} %param.12), kind=kOutput, calls=%fused_computation.2 | convolution fusion | flops 7250115072 | bytes 18880512 | tf_op jit(solution)/shard_map/dot_general | solution.py:342
  22.5 6.1 %copy.20.q_ref = f32[1536,768]{1,0:T(8,128)} copy(f32[1536,768]{0,1:T(8,128)} %get-tuple-element.50) | data formatting | bytes 9437184 | tf_op jit(solution)/shard_map/dot_general | solution.py:342
  28.7 5.2 multiply_reduce_fusion.1
  34.0 1.7 copy.21.k_ref
  37.6 9.1 %exchange_tp.1 = f32[24,128]{1,0:T(8,128)} custom-call(f32[24,128]{1,0:T(8,128)} %reshape.117.x_ref), custom_call_target="tpu_custom_call" | custom-call | flops 8000000 | bytes 24576 | tf_op jit(solution)/shard_map/exchange_tp/pallas_call | solution.py:67
  47.5 2.8 fusion
  50.3 1.6 pad_maximum_fusion.3
  54.2 7.1 %norm_rope.1 = (bf16[1536,768]{1,0:T(8,128)(2,1)}, bf16[1536,256]{1,0:T(8,128)(2,1)}) custom-call(f32[1536,768]{1,0:T(8,128)} %copy.20.q_ref, f32[1536,256]{1,0:T(8,128)} %copy.21.k_ref, f32[1536,128]{1,0:T(8,128)} %broadcast_in_dim.31.q_inv, f32[1536,128]{1,0:T(8,128)} %broadcast_in_dim.32.k_inv, f32[1,768]{1,0:T(1,128)} %reshape.130.q_gain, ...), custom_call_target="tpu_custom_call" | custom-call | flops 9437184 | bytes 9437184 | tf_op jit(solution)/shard_map/norm_rope/pallas_call | solution.py:99
  61.3 25.5 %all-gather.5.cloned.1.call-done = bf16[3072,3072]{1,0:T(8,128)(2,1)} async-done(((bf16[96,3072]{1,0:T(8,128)(2,1)}), bf16[3072,3072]{1,0:T(8,128)(2,1)}) %all-gather.5.cloned.1.call-update) | async-done | bytes 18874384 | tf_op jit(solution)/shard_map/all_gather | solution.py:340
  86.8 3.2 fusion.1
  92.4 7.2 %convolution_convert_fusion = bf16[1536,256]{1,0:T(8,128)(2,1)} fusion(bf16[1536,3072]{1,0:T(8,128)(2,1)} %bitcast.57, bf16[3072,256]{1,0:T(8,128)(2,1)S(1)} %copy-done.8), kind=kOutput, calls=%fused_computation.6 | convolution fusion | flops 2416312320 | bytes 11796480 | tf_op jit(solution)/shard_map/dot_general | solution.py:344
  99.6 19.3 %copy_bitcast_fusion = (bf16[24,2,1024,128]{3,2,1,0:T(8,128)(2,1)}, bf16[24,2,1024,128]{3,2,1,0:T(8,128)(2,1)}) fusion(bf16[24,1024,2,128]{3,2,1,0:T(2,128)(2,1)} %param.20, bf16[24,1024,2,128]{3,2,1,0:T(2,128)(2,1)} %param.19), kind=kLoop, calls=%fused_computation | loop fusion | bytes 50331648 | tf_op jit(solution)/shard_map/transpose | solution.py:360
  118.9 8.7 %all-gather.11.cloned.1.call-done.q_ref = bf16[8,8,64,768]{3,2,1,0:T(8,128)(2,1)} async-done(((bf16[1,8,64,768]{3,2,1,0:T(8,128)(2,1)}), bf16[8,8,64,768]{3,2,1,0:T(8,128)(2,1)}) %all-gather.11.cloned.1.call-update) | async-done | bytes 6291472 | tf_op jit(solution)/shard_map/all_gather | solution.py:366
  127.6 47.0 %attention.5 = (f32[8,2,6,128,256]{4,3,2,1,0:T(8,128)}, f32[8,2,8,256]{3,2,1,0:T(8,128)}, f32[8,2,8,256]{3,2,1,0:T(8,128)}) custom-call(s32[25]{0:T(128)} %pad_add_fusion.info, bf16[8,8,64,768]{3,2,1,0:T(8,128)(2,1)} %all-gather.11.cloned.1.call-done.q_ref, bf16[24,2,1024,128]{3,2,1,0:T(8,128)(2,1)} %get-tuple-element.54.k_ref, ...), custom_call_target="tpu_custom_call" | custom-call | flops 27380416512 | bytes 3342336 | tf_op jit(solution)/shard_map/attention/pallas_call | solution.py:203
  174.6 27.7 %exchange_cp.5 = f32[128,256]{1,0:T(8,128)} custom-call(f32[128,256]{1,0:T(8,128)} %bitcast.88), custom_call_target="tpu_custom_call" | custom-call | flops 8000000 | bytes 262144 | tf_op jit(solution)/shard_map/exchange_cp/pallas_call | solution.py:67
  202.3 12.8 %scale_parts.5 = f32[8,512,768]{2,1,0:T(8,128)} custom-call(f32[8,2,6,128,256]{4,3,2,1,0:T(8,128)} %get-tuple-element.29.num_ref, f32[8,2,8,256]{3,2,1,0:T(8,128)} %get-tuple-element.30.max_ref, f32[8,2,8,256]{3,2,1,0:T(8,128)} %bitcast.81), custom_call_target="tpu_custom_call" | custom-call | flops 6291456 | bytes 25165824 | tf_op jit(solution)/shard_map/scale_parts/pallas_call | solution.py:250
  215.3 47.1 %attention.4 = (f32[8,2,6,128,256]{4,3,2,1,0:T(8,128)}, f32[8,2,8,256]{3,2,1,0:T(8,128)}, f32[8,2,8,256]{3,2,1,0:T(8,128)}) custom-call(s32[25]{0:T(128)} %pad_add_fusion.info, bf16[8,8,64,768]{3,2,1,0:T(8,128)(2,1)} %all-gather.9.cloned.1.call-done.q_ref, bf16[24,2,1024,128]{3,2,1,0:T(8,128)(2,1)} %get-tuple-element.54.k_ref, ...), custom_call_target="tpu_custom_call" | custom-call | flops 27380416512 | bytes 3342336 | tf_op jit(solution)/shard_map/attention/pallas_call | solution.py:203
  262.4 22.9 %exchange_cp.4 = f32[128,256]{1,0:T(8,128)} custom-call(f32[128,256]{1,0:T(8,128)} %bitcast.89), custom_call_target="tpu_custom_call" | custom-call | flops 8000000 | bytes 262144 | tf_op jit(solution)/shard_map/exchange_cp/pallas_call | solution.py:67
  285.4 12.8 %scale_parts.4 = f32[8,512,768]{2,1,0:T(8,128)} custom-call(f32[8,2,6,128,256]{4,3,2,1,0:T(8,128)} %get-tuple-element.26.num_ref, f32[8,2,8,256]{3,2,1,0:T(8,128)} %get-tuple-element.27.max_ref, f32[8,2,8,256]{3,2,1,0:T(8,128)} %bitcast.82), custom_call_target="tpu_custom_call" | custom-call | flops 6291456 | bytes 25165824 | tf_op jit(solution)/shard_map/scale_parts/pallas_call | solution.py:250
  298.2 8.8 %reduce-scatter.4.cloned.1.call-start = ((), (), s32[]{:S(2)}) async-start(), calls=%async_computation.5 | async-start | bytes 14155776 | tf_op jit(solution)/shard_map/reduce_scatter | solution.py:372
  307.0 47.1 %attention.3 = (f32[8,2,6,128,256]{4,3,2,1,0:T(8,128)}, f32[8,2,8,256]{3,2,1,0:T(8,128)}, f32[8,2,8,256]{3,2,1,0:T(8,128)}) custom-call(s32[25]{0:T(128)} %pad_add_fusion.info, bf16[8,8,64,768]{3,2,1,0:T(8,128)(2,1)} %all-gather.7.cloned.1.call-done.q_ref, bf16[24,2,1024,128]{3,2,1,0:T(8,128)(2,1)} %get-tuple-element.54.k_ref, ...), custom_call_target="tpu_custom_call" | custom-call | flops 27380416512 | bytes 3342336 | tf_op jit(solution)/shard_map/attention/pallas_call | solution.py:203
  354.2 22.9 %exchange_cp.3 = f32[128,256]{1,0:T(8,128)} custom-call(f32[128,256]{1,0:T(8,128)} %bitcast.87), custom_call_target="tpu_custom_call" | custom-call | flops 8000000 | bytes 262144 | tf_op jit(solution)/shard_map/exchange_cp/pallas_call | solution.py:67
  377.1 12.8 %scale_parts.3 = f32[8,512,768]{2,1,0:T(8,128)} custom-call(f32[8,2,6,128,256]{4,3,2,1,0:T(8,128)} %get-tuple-element.23.num_ref, f32[8,2,8,256]{3,2,1,0:T(8,128)} %get-tuple-element.24.max_ref, f32[8,2,8,256]{3,2,1,0:T(8,128)} %bitcast.83), custom_call_target="tpu_custom_call" | custom-call | flops 6291456 | bytes 25165824 | tf_op jit(solution)/shard_map/scale_parts/pallas_call | solution.py:250
  390.0 1.6 convert_bitcast_fusion.2
  391.6 2.5 collective-permute-start
  394.2 16.1 %collective-permute-done = bf16[512,768]{1,0:T(8,128)(2,1)S(1)} collective-permute-done((bf16[512,768]{1,0:T(8,128)(2,1)S(1)}, bf16[512,768]{1,0:T(8,128)(2,1)S(1)}, u32[]{:S(2)}, u32[]{:S(2)}) %collective-permute-start) | collective-permute-done | bytes 786464 | tf_op jit(solution)/shard_map/ppermute | solution.py:318
  410.3 3.6 collective-permute-start.3
  415.6 6.8 %collective-permute-done.3 = bf16[256,768]{1,0:T(8,128)(2,1)} collective-permute-done((bf16[256,768]{1,0:T(8,128)(2,1)S(1)}, bf16[256,768]{1,0:T(8,128)(2,1)}, u32[]{:S(2)}, u32[]{:S(2)}) %collective-permute-start.3) | collective-permute-done | bytes 393248 | tf_op jit(solution)/shard_map/ppermute | solution.py:320
  422.4 4.8 collective-permute-done.2
  428.3 1.9 pad_maximum_fusion.refs_0_
  430.1 19.8 %project_out.3.refs_4_ = bf16[1536,3072]{1,0:T(8,128)(2,1)} custom-call(s32[1]{0:T(128)} %bitcast.info, bf16[4,512,768]{2,1,0:T(8,128)(2,1)} %pad_maximum_fusion.refs_0_, bf16[4,768,3072]{2,1,0:T(8,128)(2,1)} %bitcast.52, bf16[1536,3072]{1,0:T(8,128)(2,1)} %bitcast.58, f32[1,3072]{1,0:T(1,128)} %bitcast.84), custom_call_target="tpu_custom_call" | custom-call | flops 9663676416 | bytes 18874368 | tf_op jit(solution)/shard_map/project_out/pallas_call | solution.py:292
  450.0 1.6 convert_element_type.34
  451.9 1.4 collective-permute-start.5
  453.3 17.6 %collective-permute-done.4 = bf16[512,768]{1,0:T(8,128)(2,1)S(1)} collective-permute-done((bf16[512,768]{1,0:T(8,128)(2,1)S(1)}, bf16[512,768]{1,0:T(8,128)(2,1)S(1)}, u32[]{:S(2)}, u32[]{:S(2)}) %collective-permute-start.4) | collective-permute-done | bytes 786464 | tf_op jit(solution)/shard_map/ppermute | solution.py:318
  470.9 1.6 collective-permute-start.7
  472.8 8.0 %collective-permute-done.7 = bf16[256,768]{1,0:T(8,128)(2,1)S(1)} collective-permute-done((bf16[256,768]{1,0:T(8,128)(2,1)S(1)}, bf16[256,768]{1,0:T(8,128)(2,1)S(1)}, u32[]{:S(2)}, u32[]{:S(2)}) %collective-permute-start.7) | collective-permute-done | bytes 393248 | tf_op jit(solution)/shard_map/ppermute | solution.py:320
  480.8 2.8 collective-permute-done.6
  483.7 1.9 pad_maximum_fusion.1.refs_0_
  485.5 19.8 %project_out.4.refs_4_ = bf16[1536,3072]{1,0:T(8,128)(2,1)} custom-call(s32[1]{0:T(128)} %bitcast.info, bf16[4,512,768]{2,1,0:T(8,128)(2,1)} %pad_maximum_fusion.1.refs_0_, bf16[4,768,3072]{2,1,0:T(8,128)(2,1)} %bitcast.53, bf16[1536,3072]{1,0:T(8,128)(2,1)} %bitcast.59, f32[1,3072]{1,0:T(1,128)} %bitcast.85, ...), custom_call_target="tpu_custom_call", output_to_operand_aliasing={{}: (5, {})} | custom-call | flops 9663676416 | bytes 18874368 | tf_op jit(solution)/shard_map/project_out/pallas_call | solution.py:292
  505.4 1.6 convert_element_type.35
  508.5 15.8 %collective-permute-done.8 = bf16[512,768]{1,0:T(8,128)(2,1)S(1)} collective-permute-done((bf16[512,768]{1,0:T(8,128)(2,1)S(1)}, bf16[512,768]{1,0:T(8,128)(2,1)S(1)}, u32[]{:S(2)}, u32[]{:S(2)}) %collective-permute-start.8) | collective-permute-done | bytes 786464 | tf_op jit(solution)/shard_map/ppermute | solution.py:318
  524.4 1.7 collective-permute-start.11
  527.2 2.7 reshape.128
  529.9 2.7 reshape.129
  532.7 3.8 collective-permute-done.10
  537.7 1.9 pad_maximum_fusion.2.refs_0_
  539.6 19.9 %project_out.5 = bf16[1536,3072]{1,0:T(8,128)(2,1)} custom-call(s32[1]{0:T(128)} %bitcast.info, bf16[4,512,768]{2,1,0:T(8,128)(2,1)} %pad_maximum_fusion.2.refs_0_, bf16[4,768,3072]{2,1,0:T(8,128)(2,1)} %bitcast.54, bf16[1536,3072]{1,0:T(8,128)(2,1)} %bitcast.60, f32[1,3072]{1,0:T(1,128)} %bitcast.86, ...), custom_call_target="tpu_custom_call", output_to_operand_aliasing={{}: (5, {})} | custom-call | flops 9663676416 | bytes 18874368 | tf_op jit(solution)/shard_map/project_out/pallas_call | solution.py:292
  (76 shorter events, 15.3 us)
Async XLA Ops:
  7.2 21.5 %copy-start = (bf16[3072,256]{1,0:T(8,128)(2,1)S(1)}, bf16[3072,256]{1,0:T(8,128)(2,1)}, u32[]{:S(2)}) copy-start(bf16[3072,256]{1,0:T(8,128)(2,1)} %param.13) | copy-start | bytes 4718596
  7.2 79.6 %all-gather.5.cloned.1.call-start = ((), (), s32[]{:S(2)}) async-start(), calls=%async_computation.3 | async-start | bytes 19464192 | tf_op jit(solution)/shard_map/all_gather | solution.py:340
  9.4 118.3 %all-gather.11.cloned.1.call-start = ((), (), s32[]{:S(2)}) async-start(), calls=%async_computation.8 | async-start | bytes 7077888 | tf_op jit(solution)/shard_map/all_gather | solution.py:366
  33.9 2.4 copy-start.6
  33.9 2.9 copy-start.9
  33.9 3.5 copy-start.7
  86.8 5.7 copy-start.8
  90.1 125.2 %all-gather.9.cloned.1.call-start = ((), (), s32[]{:S(2)}) async-start(), calls=%async_computation.6 | async-start | bytes 7077888 | tf_op jit(solution)/shard_map/all_gather | solution.py:366
  90.9 216.2 %all-gather.7.cloned.1.call-start = ((), (), s32[]{:S(2)}) async-start(), calls=%async_computation.4 | async-start | bytes 7077888 | tf_op jit(solution)/shard_map/all_gather | solution.py:366
  91.5 298.5 %reduce-scatter.8.cloned.1.call-start = ((), (), s32[]{:S(2)}) async-start(), calls=%async_computation.9 | async-start | bytes 14155776 | tf_op jit(solution)/shard_map/reduce_scatter | solution.py:372
  215.2 234.8 %reduce-scatter.6.cloned.1.call-start = ((), (), s32[]{:S(2)}) async-start(), calls=%async_computation.7 | async-start | bytes 14155776 | tf_op jit(solution)/shard_map/reduce_scatter | solution.py:372
  298.2 207.1 %reduce-scatter.4.cloned.1.call-start = ((), (), s32[]{:S(2)}) async-start(), calls=%async_computation.5 | async-start | bytes 14155776 | tf_op jit(solution)/shard_map/reduce_scatter | solution.py:372
  390.0 24.9 %copy-start.5 = (bf16[3072]{0:T(1024)(128)(2,1)S(1)}, bf16[3072]{0:T(1024)(128)(2,1)}, u32[]{:S(2)}) copy-start(bf16[3072]{0:T(1024)(128)(2,1)} %param.18) | copy-start | bytes 18436
  390.0 25.5 %copy-start.4 = (f32[1,512,768]{2,1,0:T(8,128)S(1)}, f32[1,512,768]{2,1,0:T(8,128)}, u32[]{:S(2)}) copy-start(f32[1,512,768]{2,1,0:T(8,128)} %reduce-scatter.8.cloned.1.call-done) | copy-start | bytes 4718596
  391.6 18.7 %collective-permute-start = (bf16[512,768]{1,0:T(8,128)(2,1)S(1)}, bf16[512,768]{1,0:T(8,128)(2,1)S(1)}, u32[]{:S(2)}, u32[]{:S(2)}) collective-permute-start(bf16[512,768]{1,0:T(8,128)(2,1)S(1)} %convert_bitcast_fusion.2), channel_id=1, source_target_pairs={{0,24},{8,0},{16,8},{24,16},{1,25},{9,1},{17,9},{25,17},{2,26},{10... | collective-permute-start | bytes 2359304 | tf_op jit(solution)/shard_map/ppermute | solution.py:318
  394.2 19.9 %collective-permute-start.1 = (bf16[512,768]{1,0:T(8,128)(2,1)S(1)}, bf16[512,768]{1,0:T(8,128)(2,1)S(1)}, u32[]{:S(2)}, u32[]{:S(2)}) collective-permute-start(bf16[512,768]{1,0:T(8,128)(2,1)S(1)} %convert_bitcast_fusion.2), channel_id=1, source_target_pairs={{0,8},{8,16},{16,24},{24,0},{1,9},{9,17},{17,25},{25,1},{2,10},{10... | collective-permute-start | bytes 2359304 | tf_op jit(solution)/shard_map/ppermute | solution.py:317
  410.3 12.1 %collective-permute-start.3 = (bf16[256,768]{1,0:T(8,128)(2,1)S(1)}, bf16[256,768]{1,0:T(8,128)(2,1)}, u32[]{:S(2)}, u32[]{:S(2)}) collective-permute-start(bf16[256,768]{1,0:T(8,128)(2,1)S(1)} %slice.50), channel_id=1, source_target_pairs={{0,24},{8,0},{16,8},{24,16},{1,25},{9,1},{17,9},{25,17},{2,26},{10... | collective-permute-start | bytes 1179656 | tf_op jit(solution)/shard_map/ppermute | solution.py:320
  414.9 12.2 %collective-permute-start.2 = (bf16[256,768]{1,0:T(8,128)(2,1)}, bf16[256,768]{1,0:T(8,128)(2,1)}, u32[]{:S(2)}, u32[]{:S(2)}) collective-permute-start(bf16[256,768]{1,0:T(8,128)(2,1)} %slice.49), channel_id=1, source_target_pairs={{0,8},{8,16},{16,24},{24,0},{1,9},{9,17},{17,25},{25,1},{2,10},{10... | collective-permute-start | bytes 1179656 | tf_op jit(solution)/shard_map/ppermute | solution.py:319
  450.0 22.7 %copy-start.3 = (f32[1,512,768]{2,1,0:T(8,128)S(1)}, f32[1,512,768]{2,1,0:T(8,128)}, u32[]{:S(2)}) copy-start(f32[1,512,768]{2,1,0:T(8,128)} %reduce-scatter.6.cloned.1.call-done) | copy-start | bytes 4718596
  451.6 19.3 %collective-permute-start.4 = (bf16[512,768]{1,0:T(8,128)(2,1)S(1)}, bf16[512,768]{1,0:T(8,128)(2,1)S(1)}, u32[]{:S(2)}, u32[]{:S(2)}) collective-permute-start(bf16[512,768]{1,0:T(8,128)(2,1)S(1)} %convert_element_type.34), channel_id=1, source_target_pairs={{0,24},{8,0},{16,8},{24,16},{1,25},{9,1},{17,9},{25,17},{2,26},{10... | collective-permute-start | bytes 2359304 | tf_op jit(solution)/shard_map/ppermute | solution.py:318
  451.9 20.6 %collective-permute-start.5 = (bf16[512,768]{1,0:T(8,128)(2,1)S(1)}, bf16[512,768]{1,0:T(8,128)(2,1)S(1)}, u32[]{:S(2)}, u32[]{:S(2)}) collective-permute-start(bf16[512,768]{1,0:T(8,128)(2,1)S(1)} %convert_element_type.34), channel_id=1, source_target_pairs={{0,8},{8,16},{16,24},{24,0},{1,9},{9,17},{17,25},{25,1},{2,10},{10... | collective-permute-start | bytes 2359304 | tf_op jit(solution)/shard_map/ppermute | solution.py:317
  470.9 9.8 %collective-permute-start.7 = (bf16[256,768]{1,0:T(8,128)(2,1)S(1)}, bf16[256,768]{1,0:T(8,128)(2,1)S(1)}, u32[]{:S(2)}, u32[]{:S(2)}) collective-permute-start(bf16[256,768]{1,0:T(8,128)(2,1)S(1)} %slice.52), channel_id=1, source_target_pairs={{0,24},{8,0},{16,8},{24,16},{1,25},{9,1},{17,9},{25,17},{2,26},{10... | collective-permute-start | bytes 1179656 | tf_op jit(solution)/shard_map/ppermute | solution.py:320
  472.6 11.0 %collective-permute-start.6 = (bf16[256,768]{1,0:T(8,128)(2,1)S(1)}, bf16[256,768]{1,0:T(8,128)(2,1)S(1)}, u32[]{:S(2)}, u32[]{:S(2)}) collective-permute-start(bf16[256,768]{1,0:T(8,128)(2,1)S(1)} %slice.51), channel_id=1, source_target_pairs={{0,8},{8,16},{16,24},{24,0},{1,9},{9,17},{17,25},{25,1},{2,10},{10... | collective-permute-start | bytes 1179656 | tf_op jit(solution)/shard_map/ppermute | solution.py:319
  505.4 27.3 %copy-start.2 = (f32[1,512,768]{2,1,0:T(8,128)S(1)}, f32[1,512,768]{2,1,0:T(8,128)}, u32[]{:S(2)}) copy-start(f32[1,512,768]{2,1,0:T(8,128)} %reduce-scatter.4.cloned.1.call-done) | copy-start | bytes 4718596
  507.0 17.4 %collective-permute-start.8 = (bf16[512,768]{1,0:T(8,128)(2,1)S(1)}, bf16[512,768]{1,0:T(8,128)(2,1)S(1)}, u32[]{:S(2)}, u32[]{:S(2)}) collective-permute-start(bf16[512,768]{1,0:T(8,128)(2,1)S(1)} %convert_element_type.35), channel_id=1, source_target_pairs={{0,24},{8,0},{16,8},{24,16},{1,25},{9,1},{17,9},{25,17},{2,26},{10... | collective-permute-start | bytes 2359304 | tf_op jit(solution)/shard_map/ppermute | solution.py:318
  507.2 18.9 %collective-permute-start.9 = (bf16[512,768]{1,0:T(8,128)(2,1)S(1)}, bf16[512,768]{1,0:T(8,128)(2,1)S(1)}, u32[]{:S(2)}, u32[]{:S(2)}) collective-permute-start(bf16[512,768]{1,0:T(8,128)(2,1)S(1)} %convert_element_type.35), channel_id=1, source_target_pairs={{0,8},{8,16},{16,24},{24,0},{1,9},{9,17},{17,25},{25,1},{2,10},{10... | collective-permute-start | bytes 2359304 | tf_op jit(solution)/shard_map/ppermute | solution.py:317
  524.4 8.3 %collective-permute-start.11 = (bf16[256,768]{1,0:T(8,128)(2,1)S(1)}, bf16[256,768]{1,0:T(8,128)(2,1)}, u32[]{:S(2)}, u32[]{:S(2)}) collective-permute-start(bf16[256,768]{1,0:T(8,128)(2,1)S(1)} %slice.54), channel_id=1, source_target_pairs={{0,24},{8,0},{16,8},{24,16},{1,25},{9,1},{17,9},{25,17},{2,26},{10... | collective-permute-start | bytes 1179656 | tf_op jit(solution)/shard_map/ppermute | solution.py:320
  527.0 9.6 %collective-permute-start.10 = (bf16[256,768]{1,0:T(8,128)(2,1)}, bf16[256,768]{1,0:T(8,128)(2,1)}, u32[]{:S(2)}, u32[]{:S(2)}) collective-permute-start(bf16[256,768]{1,0:T(8,128)(2,1)} %slice.53), channel_id=1, source_target_pairs={{0,8},{8,16},{16,24},{24,0},{1,9},{9,17},{17,25},{25,1},{2,10},{10... | collective-permute-start | bytes 1179656 | tf_op jit(solution)/shard_map/ppermute | solution.py:319
  539.6 19.9 %copy-start.1 = (bf16[3072,256]{1,0:T(8,128)(2,1)S(1)}, bf16[3072,256]{1,0:T(8,128)(2,1)}, u32[]{:S(2)}) copy-start(bf16[3072,256]{1,0:T(8,128)(2,1)} %param.13) | copy-start | bytes 4718596
Sparse Core Ops, SparseCore 0:
  10.1 76.6 all-gather.4
  90.2 37.4 all-gather.10
  129.8 38.2 all-gather.8
  169.5 48.4 all-gather.6
  220.2 79.8 reduce-scatter.7
  302.2 80.7 reduce-scatter.5
  390.1 68.7 reduce-scatter.3
